TPU v7x, 32 devices: a whole 2x2x4 slice. The times are simulated.
32 devices in a mesh: gx: 4 (over z), gy: 4 (over y, x), gz: 2 (over core).
Axes of the slice: x: 2, y: 2, z: 4, core: 2. Of those that a mesh axis runs over, the one named last changes fastest.
Arguments:
- factor_inv: bfloat16 [4, 4096, 2048], P('gx', 'gy', 'gz')
- sep_sizes: int32 [4, 4, 2], P('gx', 'gy', 'gz'), may hold values from 512 to 1024
- coupling: bfloat16 [12, 4096, 2048], P('gx', 'gy', 'gz'), may hold values from -0.109375 to 0.109375
Outputs:
- schur_update: float32 [4, 4096, 2048], P('gx', 'gy', 'gz')
All inputs are finite; a program needn't handle non-finite values.
Results may differ from a plain program's by a relative error of at most 0.0023.
Values may be sent and summed in bfloat16 or wider, within the bound.
A program may use at most 128 MiB of HBM per device.

v0:
```python
import jax
import jax.numpy as jnp
from jax import lax
from jax.sharding import PartitionSpec as P


def padded(cells, sides, width):
    for axis, dim in sides:
        count = lax.axis_size(axis)
        ends = count - 1
        head = lax.slice_in_dim(cells, 0, width, axis=dim)
        tail = lax.slice_in_dim(cells, cells.shape[dim] - width, cells.shape[dim], axis=dim)
        cells = jnp.concatenate(
            [
                lax.ppermute(tail, axis, [(i, (i + 1) % count) for i in range(ends)]),
                cells,
                lax.ppermute(head, axis, [((i + 1) % count, i) for i in range(ends)]),
            ],
            axis=dim,
        )
    return cells


def passed_along(block, axis, distance):
    devices = range(lax.axis_size(axis))
    route = [(i - distance, i) for i in devices if i - distance in devices]
    return lax.ppermute(block, axis, route)


def square_of(solved):
    return lax.dot_general(
        solved, solved, (((0,), (0,)), ((), ())), preferred_element_type=jnp.float32
    )


def update_of(factor, couple):
    solved = jnp.dot(factor, couple, preferred_element_type=jnp.float32).astype(jnp.bfloat16)
    return square_of(solved)


def on_device(factor_inv, sep_sizes, coupling):
    width = factor_inv.shape[1]
    inner = jnp.arange(width, dtype=jnp.int32)
    keep = (inner < sep_sizes[0, 0, 0]).astype(jnp.bfloat16)
    masked = factor_inv[0] * keep[:, None] * keep[None, :]
    beside_all = padded(masked[None], (("gz", 0),), 1)
    below_z = beside_all[0]
    above_z = beside_all[2]
    below_y = passed_along(masked, "gy", 1)
    total = update_of(below_z, coupling[0])
    total = total + update_of(above_z, coupling[1])
    total = total + update_of(below_y, coupling[2])
    return total[None]


def solution(mesh):
    return jax.shard_map(
        on_device,
        mesh=mesh,
        in_specs=(P("gx", "gy", "gz"), P("gx", "gy", "gz"), P("gx", "gy", "gz")),
        out_specs=P("gx", "gy", "gz"),
        check_vma=False,
    )
```

profile of v0, /device:TPU:4, one launch (start us, length us, event | category | flops | bytes accessed | tf_op | source)
XLA Modules:
  0.0 82.1 jit_solution(2933055224172728530)
XLA Ops:
  0.7 0.0 copy-start
  0.7 2.0 %multiply_multiply_fusion = bf16[1,1024,1024]{2,1,0:T(8,128)(2,1)S(1)} fusion(bf16[1,1024,1024]{2,1,0:T(8,128)(2,1)} %param.3, bf16[1024]{0:T(1024)(128)(2,1)S(1)} %fusion.24), kind=kLoop, calls=%fused_computation.20 | loop fusion | flops 2097152 | bytes 4196352 | tf_op jit(solution)/shard_map/mul | solution.py:45
  2.7 1.3 %collective-permute-start.1 = (bf16[1,1024,1024]{2,1,0:T(8,128)(2,1)S(1)}, bf16[1,1024,1024]{2,1,0:T(8,128)(2,1)S(1)}, u32[]{:S(2)}, u32[]{:S(2)}) collective-permute-start(bf16[1,1024,1024]{2,1,0:T(8,128)(2,1)S(1)} %multiply_multiply_fusion), channel_id=1, source_target_pairs={{1,0},{3,2},{5,4},{7,6},{9,8},{11,10},{13,12},{15,14},{17,16},{19,... | collective-permute-start | bytes 6291464 | tf_op jit(solution)/shard_map/ppermute | solution.py:17
  4.0 0.0 copy-done
  4.0 0.3 fusion.2
  4.2 3.4 %collective-permute-start.2 = (bf16[1024,1024]{1,0:T(8,128)(2,1)S(1)}, bf16[1024,1024]{1,0:T(8,128)(2,1)}, u32[]{:S(2)}, u32[]{:S(2)}) collective-permute-start(bf16[1024,1024]{1,0:T(8,128)(2,1)S(1)} %fusion.2), channel_id=1, source_target_pairs={{0,2},{2,4},{4,6},{1,3},{3,5},{5,7},{8,10},{10,12},{12,14},{9,11},... | collective-permute-start | bytes 6291464 | tf_op jit(solution)/shard_map/ppermute | solution.py:27
  7.7 4.2 %collective-permute-start = (bf16[1,1024,1024]{2,1,0:T(8,128)(2,1)S(1)}, bf16[1,1024,1024]{2,1,0:T(8,128)(2,1)}, u32[]{:S(2)}, u32[]{:S(2)}) collective-permute-start(bf16[1,1024,1024]{2,1,0:T(8,128)(2,1)S(1)} %multiply_multiply_fusion), channel_id=1, source_target_pairs={{0,1},{2,3},{4,5},{6,7},{8,9},{10,11},{12,13},{14,15},{16,17},{18,... | collective-permute-start | bytes 6291464 | tf_op jit(solution)/shard_map/ppermute | solution.py:15
  11.9 0.0 collective-permute-done.1
  11.9 3.9 %fusion.3 = bf16[1024,1024]{1,0:T(8,128)(2,1)S(1)} fusion(bf16[1,1024,1024]{2,1,0:T(8,128)(2,1)S(1)} %collective-permute-done.1, bf16[3,1024,1024]{2,1,0:T(8,128)(2,1)} %param.5), kind=kOutput, calls=%fused_computation.5 | convolution fusion | flops 2147483648 | bytes 6291456 | tf_op jit(solution)/shard_map/dot_general | solution.py:37
  15.8 4.4 %fusion.29 = f32[1024,1024]{1,0:T(8,128)} fusion(bf16[1024,1024]{1,0:T(8,128)(2,1)S(1)} %fusion.3), kind=kOutput, calls=%fused_computation.23 | convolution fusion | flops 2147483648 | bytes 6291456 | tf_op jit(solution)/shard_map/dot_general | solution.py:31
  20.2 35.2 %collective-permute-done.2 = bf16[1024,1024]{1,0:T(8,128)(2,1)} collective-permute-done((bf16[1024,1024]{1,0:T(8,128)(2,1)S(1)}, bf16[1024,1024]{1,0:T(8,128)(2,1)}, u32[]{:S(2)}, u32[]{:S(2)}) %collective-permute-start.2) | collective-permute-done | bytes 2097184 | tf_op jit(solution)/shard_map/ppermute | solution.py:27
  55.4 12.2 %fusion.9 = f32[1024,1024]{1,0:T(8,128)} fusion(bf16[1024,1024]{1,0:T(8,128)(2,1)} %collective-permute-done.2, bf16[3,1024,1024]{2,1,0:T(8,128)(2,1)} %param.5), kind=kOutput, calls=%fused_computation.11 | convolution fusion | flops 4296015872 | bytes 8388608 | tf_op jit(solution)/shard_map/dot_general | solution.py:31
  67.5 0.0 collective-permute-done
  67.5 14.6 %add_bitcast_fusion = f32[1,1024,1024]{2,1,0:T(8,128)} fusion(f32[1024,1024]{1,0:T(8,128)} %fusion.9, f32[1024,1024]{1,0:T(8,128)} %fusion.29, bf16[1,1024,1024]{2,1,0:T(8,128)(2,1)} %collective-permute-done, bf16[3,1024,1024]{2,1,0:T(8,128)(2,1)} %param.5), kind=kOutput, calls=%fused_computation | convolution fusion | flops 4297064448 | bytes 16777216 | tf_op jit(solution)/shard_map/dot_general | solution.py:31
  (1 shorter events, 0.0 us)
Async XLA Ops:
  0.7 3.3 %copy-start = (bf16[1,1024,1024]{2,1,0:T(8,128)(2,1)S(1)}, bf16[1,1024,1024]{2,1,0:T(8,128)(2,1)}, u32[]{:S(2)}) copy-start(bf16[1,1024,1024]{2,1,0:T(8,128)(2,1)} %param.3) | copy-start | bytes 6291460
  2.7 9.2 %collective-permute-start.1 = (bf16[1,1024,1024]{2,1,0:T(8,128)(2,1)S(1)}, bf16[1,1024,1024]{2,1,0:T(8,128)(2,1)S(1)}, u32[]{:S(2)}, u32[]{:S(2)}) collective-permute-start(bf16[1,1024,1024]{2,1,0:T(8,128)(2,1)S(1)} %multiply_multiply_fusion), channel_id=1, source_target_pairs={{1,0},{3,2},{5,4},{7,6},{9,8},{11,10},{13,12},{15,14},{17,16},{19,... | collective-permute-start | bytes 6291464 | tf_op jit(solution)/shard_map/ppermute | solution.py:17
  4.2 51.1 %collective-permute-start.2 = (bf16[1024,1024]{1,0:T(8,128)(2,1)S(1)}, bf16[1024,1024]{1,0:T(8,128)(2,1)}, u32[]{:S(2)}, u32[]{:S(2)}) collective-permute-start(bf16[1024,1024]{1,0:T(8,128)(2,1)S(1)} %fusion.2), channel_id=1, source_target_pairs={{0,2},{2,4},{4,6},{1,3},{3,5},{5,7},{8,10},{10,12},{12,14},{9,11},... | collective-permute-start | bytes 6291464 | tf_op jit(solution)/shard_map/ppermute | solution.py:27
  7.7 59.9 %collective-permute-start = (bf16[1,1024,1024]{2,1,0:T(8,128)(2,1)S(1)}, bf16[1,1024,1024]{2,1,0:T(8,128)(2,1)}, u32[]{:S(2)}, u32[]{:S(2)}) collective-permute-start(bf16[1,1024,1024]{2,1,0:T(8,128)(2,1)S(1)} %multiply_multiply_fusion), channel_id=1, source_target_pairs={{0,1},{2,3},{4,5},{6,7},{8,9},{10,11},{12,13},{14,15},{16,17},{18,... | collective-permute-start | bytes 6291464 | tf_op jit(solution)/shard_map/ppermute | solution.py:15
where the time goes:
time: 82.6 us; the launch traced here: 82.1 us
  waiting for transfers between devices  35.2 us (43%)
  matrix products  35 us (42%)
  starting transfers between devices  8.92 us (11%)
  other arithmetic  2.24 us (3%)
    ppermute x1, waiting for transfers between devices, passed_along(): return lax.ppermute(block, axis, route)  35.2 us
    dot_general x3, matrix products, square_of(): lax.dot_general(solved, solved, (((0,), (0,)), ((), ())), preferred_eleme...  31.1 us
    ppermute x1, starting transfers between devices, padded(): lax.ppermute(tail, axis, [(i, (i + 1) % count) for i in range(ends)])  4.23 us
    dot_general x1, matrix products, update_of(): jnp.dot(factor, couple, preferred_element_type=jnp.float32)  3.93 us
    ppermute x1, starting transfers between devices, passed_along(): return lax.ppermute(block, axis, route)  3.4 us
    mul x2, other arithmetic, on_device(): masked = factor_inv[0] * keep[:, None] * keep[None, :]  2.24 us
  transfers between devices with their start and end apart: 3, of which 1 were waited for; matrix products, arithmetic and copies ran while one was open for 25% of the time, Pallas kernels for 0%

commit v1 on v0

v1 whole, which is shorter than its diff:
```python
import functools

import jax
import jax.numpy as jnp
from jax import lax
from jax.experimental import pallas as pl
from jax.experimental.pallas import tpu as pltpu
from jax.sharding import PartitionSpec as P

MESH = pl.DeviceIdType.MESH
F32, BF16 = jnp.float32, jnp.bfloat16
DIAG = 16
TAIL = 128


def dot(lhs, rhs, left, right):
    return lax.dot_general(lhs, rhs, (((left,), (right,)), ((), ())), preferred_element_type=F32)


def split(value):
    high = value.astype(BF16)
    return high, (value - high.astype(F32)).astype(BF16)


def gather_kernel(
    ny, nz, pieces,
    sizes, factor, coupling,
    part_out, tail_out,
    own, couple, beside, solved, total, packed, cross, packed_in, cross_in, full, lows,
    load_sem, z_send, z_recv, y_send, y_recv, store_sem,
):
    width = own.shape[0]
    half = width // 2
    block = half // 2
    steps = width // block
    b, c = lax.axis_index("gy"), lax.axis_index("gz")
    above, below = b < ny - 1, b > 0
    ups, downs = c < nz - 1, c > 0
    peers = ((above, {"gy": b + 1}), (below, {"gy": b - 1}), (ups, {"gz": c + 1}), (downs, {"gz": c - 1}))

    load_factor = pltpu.make_async_copy(factor.at[0], own, load_sem.at[3])
    load_factor.start()
    loads = [pltpu.make_async_copy(coupling.at[e], couple.at[e], load_sem.at[e]) for e in range(3)]
    for load in loads:
        load.start()

    barrier = pltpu.get_barrier_semaphore()
    for there, peer in peers:
        @pl.when(there)
        def _():
            pl.semaphore_signal(barrier, inc=1, device_id=peer, device_id_type=MESH)

    load_factor.wait()
    size = sizes[0, 0, 0]
    column = lax.broadcasted_iota(jnp.int32, (1, width), 1) < size
    diag = jnp.zeros((1, width), F32)
    for s in range(steps):
        rows = pl.ds(s * block, block)
        row = lax.broadcasted_iota(jnp.int32, (block, 1), 0) + s * block < size
        kept = own[rows, :].astype(F32) * row.astype(F32) * column.astype(F32)
        own[rows, :] = kept.astype(BF16)
        diag = diag + jnp.sum(kept * kept, axis=0, keepdims=True)

    pl.semaphore_wait(barrier, sum(there.astype(jnp.int32) for there, _ in peers))

    z_copies = []
    for k, (goes, to, comes) in enumerate(((ups, c + 1, downs), (downs, c - 1, ups))):
        copy = pltpu.make_async_remote_copy(
            src_ref=own, dst_ref=beside.at[k if nz > 2 else 0], send_sem=z_send.at[k], recv_sem=z_recv.at[k],
            device_id={"gz": to}, device_id_type=MESH,
        )
        z_copies.append((goes, comes, copy))

        @pl.when(goes)
        def _():
            copy.start()

    def y_copy(src, dst, k):
        return pltpu.make_async_remote_copy(
            src_ref=src, dst_ref=dst, send_sem=y_send.at[k], recv_sem=y_recv.at[k],
            device_id={"gy": b + 1}, device_id_type=MESH,
        )

    y_copies = [y_copy(packed, packed_in, 0)]
    for k, (start, count) in enumerate(pieces):
        rows = pl.ds(start, count)
        dst = cross_in.at[rows] if k < len(pieces) - 1 else tail_out
        y_copies.append(y_copy(cross.at[rows], dst, k + 1))

    @pl.when(above)
    def _():
        line = lax.broadcasted_iota(jnp.int32, (DIAG, half), 0)
        high = diag.astype(BF16).astype(F32)
        low = diag - high
        rows = (high[:, :half], high[:, half:], low[:, :half], low[:, half:])
        lines = jnp.zeros((DIAG, half), F32)
        for i, value in enumerate(rows):
            lines = jnp.where(line == i, value, lines)
        packed[pl.ds(half, DIAG), :] = lines.astype(BF16)
        for s in range(2):
            rows = lax.broadcasted_iota(jnp.int32, (block, half), 0) + s * block
            cols = lax.broadcasted_iota(jnp.int32, (block, half), 1)
            first = dot(own[:, pl.ds(s * block, block)], own[:, :half], 0, 0)
            second = dot(own[:, pl.ds(half + s * block, block)], own[:, half:], 0, 0)
            mixed = jnp.where(rows < cols, first, jnp.where(rows > cols, second, 0.0))
            packed[pl.ds(s * block, block), :] = mixed.astype(BF16)
        y_copies[0].start()
        for k, (start, count) in enumerate(pieces):
            cross[pl.ds(start, count), :] = dot(own[:, pl.ds(start, count)], own[:, half:], 0, 0).astype(BF16)
            y_copies[k + 1].start()

    for load in loads:
        load.wait()

    def z_slot(slot, k, fresh):
        @pl.loop(0, steps)
        def _(s):
            at = pl.ds(pl.multiple_of(s * block, block), block)
            solved[at, :] = dot(couple[slot, :, at], beside[k], 0, 1).astype(BF16)

        @pl.loop(0, steps)
        def _(s):
            at = pl.ds(pl.multiple_of(s * block, block), block)
            term = dot(solved[at, :], solved[...], 1, 1)
            total[at, :] = term if fresh else total[at, :] + term

    if nz == 2:
        for goes, comes, copy in z_copies:
            @pl.when(comes)
            def _():
                copy.wait_recv()
        z_slot(1 - c, 0, True)
    else:
        total[...] = jnp.zeros_like(total)
        for k, (goes, comes, copy) in enumerate(z_copies):
            @pl.when(comes)
            def _():
                copy.wait_recv()
                z_slot(k, k, False)

    stores = [
        pltpu.make_async_copy(
            total.at[pl.ds(s * block, block)], part_out.at[pl.ds(s * block, block)], store_sem.at[s]
        )
        for s in range(steps)
    ]

    @pl.when(below)
    def _():
        y_copies[0].wait_recv()
        rows = lax.broadcasted_iota(jnp.int32, (half, half), 0)
        cols = lax.broadcasted_iota(jnp.int32, (half, half), 1)
        mixed = packed_in[:half, :].astype(F32)
        lines = packed_in[pl.ds(half, DIAG), :].astype(F32)
        for i, keep in enumerate((rows < cols, rows > cols)):
            one = jnp.where(keep, mixed, 0.0)
            both = one + one.T + jnp.where(rows == cols, lines[i : i + 1, :], 0.0)
            full[i] = both.astype(BF16)
            lows[i] = jnp.where(rows == cols, lines[i + 2 : i + 3, :], 0.0).astype(BF16)

        @pl.loop(0, steps)
        def _(s):
            at = pl.ds(pl.multiple_of(s * block, block), block)
            term = total[at, :]
            for i in range(2):
                piece = couple[2, pl.ds(i * half, half), at]
                high, low = split(dot(piece, full[i], 0, 0) + dot(piece, lows[i], 0, 0))
                rest = couple[2, pl.ds(i * half, half), :]
                term = term + dot(high, rest, 1, 0) + dot(low, rest, 1, 0)
            total[at, :] = term

        for k, (start, count) in enumerate(pieces[:-1]):
            y_copies[k + 1].wait_recv()
            rows = pl.ds(start, count)
            high, low = split(dot(cross_in[rows, :], couple[2, pl.ds(half, half), :], 1, 0))
            mine = couple[2, rows, :]
            for i, value in enumerate((mine, mine, high, low)):
                solved[pl.ds(i * count, count), :] = value
            last = k == len(pieces) - 2
            for s in range(steps):
                at = pl.ds(s * block, block)
                term = dot(solved[pl.ds(0, 2 * count), at], solved[pl.ds(2 * count, 2 * count), :], 0, 0)
                term = term + dot(solved[pl.ds(2 * count, 2 * count), at], solved[pl.ds(0, 2 * count), :], 0, 0)
                total[at, :] = total[at, :] + term
                if last:
                    stores[s].start()

    @pl.when(jnp.logical_not(below))
    def _():
        for store in stores:
            store.start()

    @pl.when(below)
    def _():
        y_copies[-1].wait_recv()

    for goes, comes, copy in z_copies:
        @pl.when(goes)
        def _():
            copy.wait_send()

    @pl.when(above)
    def _():
        for copy in y_copies:
            copy.wait_send()

    for store in stores:
        store.wait()


def finish_kernel(tail, mine, rest, part, out, left, right):
    count = tail.shape[0]

    @pl.when(pl.program_id(0) == 0)
    def _():
        held = jnp.where(lax.axis_index("gy") > 0, tail[...].astype(F32), 0.0).astype(BF16)
        high, low = split(dot(held, rest[0], 1, 0))
        for i, (one, other) in enumerate(((mine[0], high), (mine[0], low), (high, mine[0]), (low, mine[0]))):
            left[pl.ds(i * count, count), :] = one
            right[pl.ds(i * count, count), :] = other

    block = out.shape[1]
    at = pl.ds(pl.multiple_of(pl.program_id(0) * block, block), block)
    out[0] = part[...] + dot(left[:, at], right[...], 0, 0)


def on_device(factor_inv, sep_sizes, coupling):
    ny, nz = lax.axis_size("gy"), lax.axis_size("gz")
    width = factor_inv.shape[1]
    inter = coupling.shape[2]
    half = width // 2
    block = half // 2
    steps = width // block
    tail = min(TAIL, block)
    pieces = [(0, block)] + [(start, tail) for start in range(block, half, tail)]
    count = len(pieces) + 1
    anywhere = pl.BlockSpec(memory_space=pl.ANY)
    part, last = pl.pallas_call(
        functools.partial(gather_kernel, ny, nz, pieces),
        out_shape=(
            jax.ShapeDtypeStruct((inter, inter), F32),
            jax.ShapeDtypeStruct((tail, half), BF16),
        ),
        in_specs=[pl.BlockSpec(memory_space=pltpu.SMEM), anywhere, anywhere],
        out_specs=(anywhere, anywhere),
        scratch_shapes=[
            pltpu.VMEM((width, width), BF16),
            pltpu.VMEM((3, width, inter), BF16),
            pltpu.VMEM((2 if nz > 2 else 1, width, width), BF16),
            pltpu.VMEM((inter, width), BF16),
            pltpu.VMEM((inter, inter), F32),
            pltpu.VMEM((half + DIAG, half), BF16),
            pltpu.VMEM((half, half), BF16),
            pltpu.VMEM((half + DIAG, half), BF16),
            pltpu.VMEM((half, half), BF16),
            pltpu.VMEM((2, half, half), BF16),
            pltpu.VMEM((2, half, half), BF16),
            pltpu.SemaphoreType.DMA((4,)),
            pltpu.SemaphoreType.DMA((2,)),
            pltpu.SemaphoreType.DMA((2,)),
            pltpu.SemaphoreType.DMA((count,)),
            pltpu.SemaphoreType.DMA((count,)),
            pltpu.SemaphoreType.DMA((steps,)),
        ],
        compiler_params=pltpu.CompilerParams(
            collective_id=0, has_side_effects=True, vmem_limit_bytes=56 * 2**20
        ),
    )(sep_sizes, factor_inv, coupling)
    rows = block
    return pl.pallas_call(
        finish_kernel,
        grid=(inter // rows,),
        out_shape=jax.ShapeDtypeStruct((1, inter, inter), F32),
        in_specs=[
            pl.BlockSpec((tail, half), lambda s: (0, 0)),
            pl.BlockSpec((1, tail, inter), lambda s: (2, half // tail - 1, 0)),
            pl.BlockSpec((1, half, inter), lambda s: (2, 1, 0)),
            pl.BlockSpec((rows, inter), lambda s: (s, 0)),
        ],
        out_specs=pl.BlockSpec((1, rows, inter), lambda s: (0, s, 0)),
        scratch_shapes=[pltpu.VMEM((4 * tail, inter), BF16), pltpu.VMEM((4 * tail, inter), BF16)],
        compiler_params=pltpu.CompilerParams(vmem_limit_bytes=56 * 2**20),
    )(last, coupling, coupling, part)


def solution(mesh):
    return jax.shard_map(
        on_device,
        mesh=mesh,
        in_specs=(P("gx", "gy", "gz"), P("gx", "gy", "gz"), P("gx", "gy", "gz")),
        out_specs=P("gx", "gy", "gz"),
        check_vma=False,
    )
```

time: 82.6 us -> 39.6 us (0.48)
  Pallas kernels: 0 us -> 38.8 us
  waiting for transfers between devices: 35.2 us -> 0 us
  matrix products: 35 us -> 0 us
  starting transfers between devices: 8.92 us -> 0 us
  other arithmetic: 2.24 us -> 0 us
    pallas_call x0 -> x2, Pallas kernels: none -> 38.8 us  [the longest x1 32.3 us: on_device(): pl.pallas_call(functools.partial(gather_kernel, ny, nz, pieces), out_shap...]
    ppermute x3 -> x0, waiting for transfers between devices: 35.2 us -> none  [the longest x1 35.2 us: passed_along(): return lax.ppermute(block, axis, route)]
    dot_general x4 -> x0, matrix products: 35 us -> none  [the longest x3 31.1 us: square_of(): lax.dot_general(solved, solved, (((0,), (0,)), ((), ())), preferred_eleme...]
    ppermute x3 -> x0, starting transfers between devices: 8.92 us -> none  [the longest x1 4.23 us: padded(): lax.ppermute(tail, axis, [(i, (i + 1) % count) for i in range(ends)])]
    mul x2 -> x0, other arithmetic: 2.24 us -> none  [on_device(): masked = factor_inv[0] * keep[:, None] * keep[None, :]]
  transfers between devices with their start and end apart: 3 -> 0, of which waited for: 1 -> 0; matrix products, arithmetic and copies ran while one was open for 25% -> 0% of each run, Pallas kernels for 0% -> 0%
where the time goes in v1:
time: 39.6 us; the launch traced here: 39.5 us
  Pallas kernels  38.8 us (98%)
  between operations  0.66 us (2%)
    pallas_call x1, Pallas kernels, on_device(): pl.pallas_call(functools.partial(gather_kernel, ny, nz, pieces), out_shap...  32.3 us
    pallas_call x1, Pallas kernels, on_device(): pl.pallas_call(finish_kernel, grid=(inter // rows,), out_shape=jax.ShapeD...  6.46 us

profile of v1, /device:TPU:4, one launch (start us, length us, event | category | flops | bytes accessed | tf_op | source)
XLA Modules:
  0.0 39.5 jit_solution(3402816281369961194)
XLA Ops:
  0.7 32.3 %shard_map.37 = (f32[1024,1024]{1,0:T(8,128)}, bf16[128,512]{1,0:T(8,128)(2,1)}) custom-call(s32[1,1,1]{2,1,0:T(1,128)S(6)} %copy.4.sizes, bf16[1,1024,1024]{2,1,0:T(8,128)(2,1)} %factor.1, bf16[3,1024,1024]{2,1,0:T(8,128)(2,1)} %rest.1), custom_call_target="tpu_custom_call" | custom-call | tf_op jit(solution)/shard_map/pallas_call | solution.py:238
  33.0 6.5 %shard_map.38 = f32[1,1024,1024]{2,1,0:T(8,128)} custom-call(bf16[128,512]{1,0:T(8,128)(2,1)} %get-tuple-element.7.tail, bf16[3,1024,1024]{2,1,0:T(8,128)(2,1)} %rest.1, bf16[3,1024,1024]{2,1,0:T(8,128)(2,1)} %rest.1, f32[1024,1024]{1,0:T(8,128)} %get-tuple-element.8.part), custom_call_target="tpu_custom_call" | custom-call | tf_op jit(solution)/shard_map/pallas_call | solution.py:270

commit v2 on v1

--- a/solution.py
+++ b/solution.py
@@ -15,11 +15,6 @@
 
 def dot(lhs, rhs, left, right):
     return lax.dot_general(lhs, rhs, (((left,), (right,)), ((), ())), preferred_element_type=F32)
-
-
-def split(value):
-    high = value.astype(BF16)
-    return high, (value - high.astype(F32)).astype(BF16)
 
 
 def gather_kernel(
@@ -38,11 +33,11 @@
     ups, downs = c < nz - 1, c > 0
     peers = ((above, {"gy": b + 1}), (below, {"gy": b - 1}), (ups, {"gz": c + 1}), (downs, {"gz": c - 1}))
 
-    load_factor = pltpu.make_async_copy(factor.at[0], own, load_sem.at[3])
-    load_factor.start()
+    rows_of = [pl.ds(s * block, block) for s in range(steps)]
+    factors = [pltpu.make_async_copy(factor.at[0, at], own.at[at], load_sem.at[3 + s]) for s, at in enumerate(rows_of)]
+    for load in factors:
+        load.start()
     loads = [pltpu.make_async_copy(coupling.at[e], couple.at[e], load_sem.at[e]) for e in range(3)]
-    for load in loads:
-        load.start()
 
     barrier = pltpu.get_barrier_semaphore()
     for there, peer in peers:
@@ -50,17 +45,19 @@
         def _():
             pl.semaphore_signal(barrier, inc=1, device_id=peer, device_id_type=MESH)
 
-    load_factor.wait()
     size = sizes[0, 0, 0]
     column = lax.broadcasted_iota(jnp.int32, (1, width), 1) < size
     diag = jnp.zeros((1, width), F32)
     for s in range(steps):
-        rows = pl.ds(s * block, block)
+        rows = rows_of[s]
+        factors[s].wait()
         row = lax.broadcasted_iota(jnp.int32, (block, 1), 0) + s * block < size
         kept = own[rows, :].astype(F32) * row.astype(F32) * column.astype(F32)
         own[rows, :] = kept.astype(BF16)
         diag = diag + jnp.sum(kept * kept, axis=0, keepdims=True)
 
+    for load in loads:
+        load.start()
     pl.semaphore_wait(barrier, sum(there.astype(jnp.int32) for there, _ in peers))
 
     z_copies = []
@@ -89,6 +86,12 @@
 
     @pl.when(above)
     def _():
+        def send_cross(k):
+            start, count = pieces[k]
+            cross[pl.ds(start, count), :] = dot(own[:, pl.ds(start, count)], own[:, half:], 0, 0).astype(BF16)
+            y_copies[k + 1].start()
+
+        send_cross(0)
         line = lax.broadcasted_iota(jnp.int32, (DIAG, half), 0)
         high = diag.astype(BF16).astype(F32)
         low = diag - high
@@ -105,9 +108,8 @@
             mixed = jnp.where(rows < cols, first, jnp.where(rows > cols, second, 0.0))
             packed[pl.ds(s * block, block), :] = mixed.astype(BF16)
         y_copies[0].start()
-        for k, (start, count) in enumerate(pieces):
-            cross[pl.ds(start, count), :] = dot(own[:, pl.ds(start, count)], own[:, half:], 0, 0).astype(BF16)
-            y_copies[k + 1].start()
+        for k in range(1, len(pieces)):
+            send_cross(k)
 
     for load in loads:
         load.wait()
@@ -164,23 +166,22 @@
             term = total[at, :]
             for i in range(2):
                 piece = couple[2, pl.ds(i * half, half), at]
-                high, low = split(dot(piece, full[i], 0, 0) + dot(piece, lows[i], 0, 0))
+                high = (dot(piece, full[i], 0, 0) + dot(piece, lows[i], 0, 0)).astype(BF16)
                 rest = couple[2, pl.ds(i * half, half), :]
-                term = term + dot(high, rest, 1, 0) + dot(low, rest, 1, 0)
+                term = term + dot(high, rest, 1, 0)
             total[at, :] = term
 
         for k, (start, count) in enumerate(pieces[:-1]):
             y_copies[k + 1].wait_recv()
             rows = pl.ds(start, count)
-            high, low = split(dot(cross_in[rows, :], couple[2, pl.ds(half, half), :], 1, 0))
+            high = dot(cross_in[rows, :], couple[2, pl.ds(half, half), :], 1, 0).astype(BF16)
             mine = couple[2, rows, :]
-            for i, value in enumerate((mine, mine, high, low)):
+            for i, value in enumerate((mine, high, mine)):
                 solved[pl.ds(i * count, count), :] = value
             last = k == len(pieces) - 2
             for s in range(steps):
                 at = pl.ds(s * block, block)
-                term = dot(solved[pl.ds(0, 2 * count), at], solved[pl.ds(2 * count, 2 * count), :], 0, 0)
-                term = term + dot(solved[pl.ds(2 * count, 2 * count), at], solved[pl.ds(0, 2 * count), :], 0, 0)
+                term = dot(solved[pl.ds(0, 2 * count), at], solved[pl.ds(count, 2 * count), :], 0, 0)
                 total[at, :] = total[at, :] + term
                 if last:
                     stores[s].start()
@@ -214,8 +215,8 @@
     @pl.when(pl.program_id(0) == 0)
     def _():
         held = jnp.where(lax.axis_index("gy") > 0, tail[...].astype(F32), 0.0).astype(BF16)
-        high, low = split(dot(held, rest[0], 1, 0))
-        for i, (one, other) in enumerate(((mine[0], high), (mine[0], low), (high, mine[0]), (low, mine[0]))):
+        high = dot(held, rest[0], 1, 0).astype(BF16)
+        for i, (one, other) in enumerate(((mine[0], high), (high, mine[0]))):
             left[pl.ds(i * count, count), :] = one
             right[pl.ds(i * count, count), :] = other
 
@@ -232,7 +233,7 @@
     block = half // 2
     steps = width // block
     tail = min(TAIL, block)
-    pieces = [(0, block)] + [(start, tail) for start in range(block, half, tail)]
+    pieces = [(start, tail) for start in range(0, half, tail)]
     count = len(pieces) + 1
     anywhere = pl.BlockSpec(memory_space=pl.ANY)
     part, last = pl.pallas_call(
@@ -255,7 +256,7 @@
             pltpu.VMEM((half, half), BF16),
             pltpu.VMEM((2, half, half), BF16),
             pltpu.VMEM((2, half, half), BF16),
-            pltpu.SemaphoreType.DMA((4,)),
+            pltpu.SemaphoreType.DMA((3 + steps,)),
             pltpu.SemaphoreType.DMA((2,)),
             pltpu.SemaphoreType.DMA((2,)),
             pltpu.SemaphoreType.DMA((count,)),
@@ -278,7 +279,7 @@
             pl.BlockSpec((rows, inter), lambda s: (s, 0)),
         ],
         out_specs=pl.BlockSpec((1, rows, inter), lambda s: (0, s, 0)),
-        scratch_shapes=[pltpu.VMEM((4 * tail, inter), BF16), pltpu.VMEM((4 * tail, inter), BF16)],
+        scratch_shapes=[pltpu.VMEM((2 * tail, inter), BF16), pltpu.VMEM((2 * tail, inter), BF16)],
         compiler_params=pltpu.CompilerParams(vmem_limit_bytes=56 * 2**20),
     )(last, coupling, coupling, part)
 

time: 39.6 us -> 37.3 us (0.942)
  Pallas kernels: 38.8 us -> 36.5 us
    pallas_call x1, Pallas kernels: 32.3 us -> 30.5 us  [on_device(): pl.pallas_call(functools.partial(gather_kernel, ny, nz, pieces), out_shap...]
    pallas_call x1, Pallas kernels: 6.46 us -> 6 us  [on_device(): pl.pallas_call(finish_kernel, grid=(inter // rows,), out_shape=jax.ShapeD...]
where the time goes in v2:
time: 37.3 us; the launch traced here: 37.1 us
  Pallas kernels  36.5 us (98%)
  between operations  0.66 us (2%)
    pallas_call x1, Pallas kernels, on_device(): pl.pallas_call(functools.partial(gather_kernel, ny, nz, pieces), out_shap...  30.5 us
    pallas_call x1, Pallas kernels, on_device(): pl.pallas_call(finish_kernel, grid=(inter // rows,), out_shape=jax.ShapeD...  6 us

profile of v2, /device:TPU:4, one launch (start us, length us, event | category | flops | bytes accessed | tf_op | source)
XLA Modules:
  0.0 37.1 jit_solution(9870028640842697873)
XLA Ops:
  0.7 30.5 %shard_map.37 = (f32[1024,1024]{1,0:T(8,128)}, bf16[128,512]{1,0:T(8,128)(2,1)}) custom-call(s32[1,1,1]{2,1,0:T(1,128)S(6)} %copy.4.sizes, bf16[1,1024,1024]{2,1,0:T(8,128)(2,1)} %factor.1, bf16[3,1024,1024]{2,1,0:T(8,128)(2,1)} %rest.1), custom_call_target="tpu_custom_call" | custom-call | tf_op jit(solution)/shard_map/pallas_call | solution.py:239
  31.1 6.0 %shard_map.38 = f32[1,1024,1024]{2,1,0:T(8,128)} custom-call(bf16[128,512]{1,0:T(8,128)(2,1)} %get-tuple-element.7.tail, bf16[3,1024,1024]{2,1,0:T(8,128)(2,1)} %rest.1, bf16[3,1024,1024]{2,1,0:T(8,128)(2,1)} %rest.1, f32[1024,1024]{1,0:T(8,128)} %get-tuple-element.8.part), custom_call_target="tpu_custom_call" | custom-call | tf_op jit(solution)/shard_map/pallas_call | solution.py:271
